TPU v7x, 32 devices: a whole 2x2x4 slice. The times are simulated.
32 devices in a mesh: grp: 2 (over y), col: 4 (over z), blk: 4 (over x, core).
Axes of the slice: x: 2, y: 2, z: 4, core: 2. Of those that a mesh axis runs over, the one named last changes fastest.
Arguments:
- boundary: bfloat16 [32, 192, 576], P(('grp', 'col'), 'blk'), parts along dimension 0, may hold values from -6 to 6
- row_tensor: bfloat16 [32, 6, 6, 6, 6], P(('grp', 'col')), parts along dimension 0, may hold values from -1.5 to 1.5
- left_proj: bfloat16 [32, 192, 576], P(('grp', 'col'), 'blk'), parts along dimension 0, may hold values from -0.75 to 0.75
- right_proj: bfloat16 [32, 192, 576], P(('grp', 'col'), 'blk'), parts along dimension 0, may hold values from -0.3125 to 0.3125
- leg_parity: int32 [32, 3, 6], P('grp'), parts along dimension 0, may hold values from 0 to 1
- bond_charges: int32 [32, 2], P('grp'), parts along dimension 0, may hold values from 32 to 96, as said below
Outputs:
- new_boundary: bfloat16 [32, 192, 576], P(('grp', 'col'), 'blk'), parts along dimension 0
There are 2 independent parts, one for each index of `grp`. A program takes and returns all parts, laid end to end along the dimension named above; each array names one. Nothing has to cross between parts.
Inputs may be any that keep to these rules, and one draw needn't show every extreme that they name: `bond_charges`: odd counts are 128 minus these, so neither block of a bond holds more than 96 live rows; some bond has an even count of 96 and some bond an odd count of 96. `leg_parity`: [c, 0] is the horizontal leg left of column c, [c, 1] the vertical leg between boundary and row, [c, 2] the outgoing vertical leg.
All inputs are finite; a program needn't handle non-finite values.
Results may differ from a plain program's by a relative error of at most 0.0057.
Values may be sent and summed in bfloat16 or wider, within the bound.
A program may use at most 64 MiB of HBM per device.

v0:
```python
import jax
import jax.numpy as jnp
from jax import lax
from jax.sharding import PartitionSpec as P

CHI = 128
BLOCK = 96
D = 6


def passed_along(x, axis, by):
    length = lax.axis_size(axis)
    return lax.ppermute(x, axis, [(i, (i + by) % length) for i in range(length)])


def live_rows(counts, parity, position):
    limit = jnp.where(parity == 0, counts, CHI - counts)
    return position < limit


def per_device(boundary, row_tensor, left_proj, right_proj, leg_parity, bond_charges):
    col_dev, sub_rows, merged = boundary.shape
    start_col = lax.axis_index("col") * col_dev
    charges_here = lax.dynamic_slice_in_dim(bond_charges, start_col, col_dev, 0)
    charges_next = lax.dynamic_slice_in_dim(jnp.roll(bond_charges, -1, 0), start_col, col_dev, 0)
    legs_here = lax.dynamic_slice_in_dim(leg_parity, start_col, col_dev, 0)
    legs_next = lax.dynamic_slice_in_dim(jnp.roll(leg_parity, -1, 0), start_col, col_dev, 0)
    in_here = charges_here[:, 0]
    out_here = charges_here[:, 1]
    in_next = charges_next[:, 0]
    out_next = charges_next[:, 1]
    left_leg = legs_here[:, 0]
    up_leg = legs_here[:, 1]
    down_leg = legs_here[:, 2]
    right_leg = legs_next[:, 0]
    inside = lax.iota(jnp.int32, BLOCK)
    row_start = lax.axis_index("blk") * sub_rows
    local_index = row_start + lax.iota(jnp.int32, sub_rows)
    local_parity = local_index // BLOCK
    local_position = local_index % BLOCK
    left_sel = (local_parity[None, :, None] + left_leg[:, None, :]) % 2
    left_mask = live_rows(out_here[:, None], local_parity[None, :], local_position[None, :])[
        :, :, None, None
    ] & live_rows(in_here[:, None, None, None], left_sel[..., None], inside[None, None, None, :])
    left_m = left_proj.reshape(col_dev, sub_rows, D, BLOCK) * left_mask.astype(jnp.bfloat16)
    left_dense = jnp.concatenate(
        [
            left_m * (left_sel == 0).astype(jnp.bfloat16)[..., None],
            left_m * (left_sel == 1).astype(jnp.bfloat16)[..., None],
        ],
        axis=3,
    )
    piece = lax.all_gather(boundary, "blk", axis=1, tiled=True)
    count_rows = piece.shape[1]
    row_index = lax.iota(jnp.int32, count_rows)
    row_parity = row_index // BLOCK
    row_position = row_index % BLOCK
    bound_sel = (row_parity[None, :, None] + up_leg[:, None, :]) % 2
    bound_mask = live_rows(in_here[:, None], row_parity[None, :], row_position[None, :])[
        :, :, None, None
    ] & live_rows(in_next[:, None, None, None], bound_sel[..., None], inside[None, None, None, :])
    piece_m = piece.reshape(col_dev, count_rows, D, BLOCK) * bound_mask.astype(jnp.bfloat16)
    absorbed = jnp.einsum(
        "cpla,caub->cplub", left_dense, piece_m, preferred_element_type=jnp.float32
    ).astype(jnp.bfloat16)
    row_keep = (
        left_leg[:, :, None, None, None]
        + up_leg[:, None, :, None, None]
        + down_leg[:, None, None, :, None]
        + right_leg[:, None, None, None, :]
    ) % 2 == 0
    row_sign = 1 - 2 * left_leg[:, :, None, None, None] * up_leg[:, None, :, None, None]
    row_m = row_tensor * jnp.where(row_keep, row_sign, 0).astype(jnp.bfloat16)
    mixed = jnp.einsum("cplub,cludr->cpdrb", absorbed, row_m, preferred_element_type=jnp.float32)
    block_par = (
        local_parity[None, :, None, None] + down_leg[:, None, :, None] + right_leg[:, None, None, :]
    ) % 2
    sign_flip = (1 - 2 * block_par * down_leg[:, None, :, None]).astype(jnp.float32)
    mixed = (mixed * sign_flip[..., None]).astype(jnp.bfloat16)
    mixed_dense = jnp.concatenate(
        [
            mixed * (block_par == 0).astype(jnp.bfloat16)[..., None],
            mixed * (block_par == 1).astype(jnp.bfloat16)[..., None],
        ],
        axis=4,
    )
    incoming = passed_along(right_proj[:1], "col", -1)
    right_next = jnp.concatenate([right_proj[1:], incoming], axis=0)
    piece = lax.all_gather(right_next, "blk", axis=1, tiled=True)
    count_rows = piece.shape[1]
    row_index = lax.iota(jnp.int32, count_rows)
    row_parity = row_index // BLOCK
    row_position = row_index % BLOCK
    right_sel = (row_parity[None, :, None] + right_leg[:, None, :]) % 2
    right_mask = live_rows(in_next[:, None], row_parity[None, :], row_position[None, :])[
        :, :, None, None
    ] & live_rows(out_next[:, None, None, None], right_sel[..., None], inside[None, None, None, :])
    piece_m = piece.reshape(col_dev, count_rows, D, BLOCK) * right_mask.astype(jnp.bfloat16)
    result = jnp.einsum(
        "cpdrb,cbre->cpde", mixed_dense, piece_m, preferred_element_type=jnp.float32
    )
    return result.astype(jnp.bfloat16).reshape(col_dev, sub_rows, merged)


def solution(mesh):
    in_specs = (
        P(("grp", "col"), "blk", None),
        P(("grp", "col"), None, None, None, None),
        P(("grp", "col"), "blk", None),
        P(("grp", "col"), "blk", None),
        P("grp", None, None),
        P("grp", None),
    )
    out_specs = P(("grp", "col"), "blk", None)
    return jax.shard_map(
        per_device, mesh=mesh, in_specs=in_specs, out_specs=out_specs, check_vma=False
    )
```

profile of v0, /device:TPU:0, one launch (start us, length us, event | category | flops | bytes accessed | tf_op | source)
XLA Modules:
  0.0 54.8 jit_solution(14372236034611323243)
XLA Ops:
  0.0 0.8 %slice.62 = bf16[1,48,576]{2,1,0:T(8,128)(2,1)S(1)} slice(bf16[4,48,576]{2,1,0:T(8,128)(2,1)} %param.9), slice={[0:1], [0:48], [0:576]} | slice | bytes 110592 | tf_op jit(solution)/shard_map/slice | solution.py:87
  0.8 5.1 %collective-permute-start = (bf16[1,48,576]{2,1,0:T(8,128)(2,1)S(1)}, bf16[1,48,576]{2,1,0:T(8,128)(2,1)S(1)}, u32[]{:S(2)}, u32[]{:S(2)}) collective-permute-start(bf16[1,48,576]{2,1,0:T(8,128)(2,1)S(1)} %slice.62), channel_id=1, source_target_pairs={{0,12},{4,0},{8,4},{12,8},{1,13},{5,1},{9,5},{13,9},{2,14},{6,2},{... | collective-permute-start | bytes 165896 | tf_op jit(solution)/shard_map/ppermute | solution.py:13
  5.9 0.7 %slice.57 = s32[15,2]{0,1:T(2,128)S(1)} slice(s32[16,2]{0,1:T(2,128)} %param.11), slice={[1:16], [0:2]} | slice | bytes 240 | tf_op jit(solution)/shard_map/jit(_roll_static)/slice | solution.py:25
  6.7 0.8 %pad_add_fusion = s32[16,2]{0,1:T(2,128)S(1)} fusion(s32[1,2]{0,1:T(2,128)} %bitcast.75, s32[15,2]{0,1:T(2,128)S(1)} %slice.57), kind=kLoop, calls=%fused_computation.102 | loop fusion | flops 32 | bytes 256 | tf_op jit(solution)/shard_map/jit(_roll_static)/concatenate | solution.py:25
  7.4 0.8 %constant_dynamic-slice_fusion.2 = (s32[4,2]{0,1:T(2,128)S(1)}, s32[4,2]{0,1:T(2,128)S(1)}) fusion(s32[16,2]{0,1:T(2,128)S(1)} %pad_add_fusion, s32[]{:T(128)S(6)} %select_n.177, s32[16,2]{0,1:T(2,128)} %param.11), kind=kLoop, calls=%fused_computation.97 | loop fusion | bytes 132 | tf_op jit(solution)/shard_map/dynamic_slice | solution.py:25
  8.3 0.8 %slice.51 = s32[15,3,6]{0,2,1:T(8,128)S(1)} slice(s32[16,3,6]{0,2,1:T(8,128)} %param.10), slice={[1:16], [0:3], [0:6]} | slice | bytes 2160 | tf_op jit(solution)/shard_map/jit(_roll_static)/slice | solution.py:27
  9.1 0.8 %constant_dynamic-slice_fusion.1 = (s32[4,1,6]{0,2,1:T(8,128)S(1)}, s32[4,1,6]{0,2,1:T(8,128)S(1)}, s32[4,1,6]{0,2,1:T(8,128)S(1)}, s32[4,1,6]{0,2,1:T(8,128)S(1)}) fusion(s32[16,3,6]{0,2,1:T(8,128)} %param.10, s32[]{:T(128)S(6)} %select_n.177, s32[]{:T(128)S(6)} %add.320, s32[]{:T(128)S(6)} %add.321, s32[1,3,6]{0,2,1:T(8,128)} %bitcast.63, ...), kind=kLoop, calls=%fused_computation.96 | loop fusion | flops 24 | bytes 1836 | tf_op jit(solution)/shard_map/slice | solution.py:32
  9.9 0.1 copy.38
  10.0 0.1 copy.42
  10.1 0.1 copy.39
  10.2 0.1 fusion.45
  10.3 1.3 %reshape.409 = bf16[4,48,6,96]{3,2,1,0:T(8,128)(2,1)S(1)} reshape(bf16[4,48,576]{2,1,0:T(8,128)(2,1)} %param.8) | data formatting | bytes 442368 | tf_op jit(solution)/shard_map/reshape | solution.py:45
  11.6 0.1 copy.44
  11.7 0.1 copy.40
  11.8 1.0 %copy.47 = bf16[4,48,576]{2,0,1:T(4,128)(2,1)S(1)} copy(bf16[4,48,576]{2,1,0:T(8,128)(2,1)} %param.6) | data formatting | bytes 442368 | tf_op args[0]
  12.8 0.0 copy-start
  12.8 9.8 %all_gather.6 = bf16[4,192,576]{2,0,1:T(4,128)(2,1)S(1)} all-gather(bf16[4,48,576]{2,0,1:T(4,128)(2,1)S(1)} %copy.47), channel_id=1, replica_groups=mesh['grp'=2,'col'=4,'blk'=4] {'blk'}, dimensions={1}, use_global_device_ids=true | all-gather | bytes 1105920 | tf_op jit(solution)/shard_map/all_gather | solution.py:53
  22.6 1.3 %copy.48 = bf16[4,192,576]{1,2,0:T(8,128)(2,1)S(1)} copy(bf16[4,192,576]{2,0,1:T(4,128)(2,1)S(1)} %all_gather.6) | data formatting | bytes 1769472 | tf_op jit(solution)/shard_map/all_gather | solution.py:53
  23.9 0.1 copy.45
  24.0 0.1 copy.41
  24.1 0.1 copy.43
  24.2 0.1 broadcast_select_fusion
  24.3 0.4 compare_convert_fusion.1
  24.7 0.4 subtract_convert_fusion
  25.1 0.0 copy-done
  25.1 0.7 %fusion.36 = bf16[4,6,6,6,6,1]{4,0,3,2,1,5:T(4,128)(2,1)S(1)} fusion(bf16[4,6,6,6,6]{4,0,3,2,1:T(4,128)(2,1)S(1)} %copy-done, s32[4,6,6]{0,2,1:T(8,128)S(1)} %get-tuple-element.15, s32[4,6]{1,0:T(4,128)S(1)} %bitcast.66, s32[4,6,6,6]{0,3,2,1:T(8,128)S(1)} %broadcast_add_fusion), kind=kLoop, calls=%fused_computation.52 | loop fusion | flops 98496 | bytes 24864 | tf_op jit(solution)/shard_map/mul | solution.py:73
  25.8 0.1 select_compare_fusion.2
  25.9 0.1 fusion.41
  26.0 0.1 select_compare_fusion
  26.1 0.6 %broadcast_multiply_fusion.3 = (bf16[4,48,6,96]{3,1,2,0:T(8,128)(2,1)S(1)}, bf16[4,48,6,96]{3,1,2,0:T(8,128)(2,1)S(1)}) fusion(bf16[4,48,6]{1,2,0:T(8,128)(2,1)S(1)} %get-tuple-element.16, bf16[4,48,6,96]{3,2,1,0:T(8,128)(2,1)S(1)} %reshape.409, s32[4,48,6]{1,2,0:T(8,128)S(1)} %get-tuple-element.31, pred[4,48]{1,0:T(4,128)(4,1)S(1)} %select_compare_fusion.2, ...), kind=kLoop, calls=%fused_computation.54 | loop fusion | flops 1105920 | bytes 672960 | tf_op jit(solution)/shard_map/mul | solution.py:48
  26.7 1.0 %convert_bitcast_fusion = bf16[4,48,6,6,96,1]{4,1,3,2,0,5:T(8,128)(2,1)S(1)} fusion(bf16[4,192,6,96]{1,3,2,0:T(8,128)(2,1)S(1)} %bitcast.61, s32[4,192,6]{1,2,0:T(8,128)S(1)} %get-tuple-element.24, pred[4,192]{1,0:T(4,128)(4,1)S(1)} %get-tuple-element.19, bf16[4,48,6,96]{3,1,2,0:T(8,128)(2,1)S(1)} %get-tuple-element.8, ...), kind=kOutput, calls=%fused_computation.13 | convolution fusion | flops 257679360 | bytes 2673408 | tf_op jit(solution)/shard_map/cpla,caub->cplub/dot_general | solution.py:63
  27.7 6.6 %broadcast_multiply_fusion.1 = (bf16[4,48,6,6,96]{4,3,1,2,0:T(8,128)(2,1)S(1)}, bf16[4,48,6,6,96]{4,3,1,2,0:T(8,128)(2,1)S(1)}) fusion(bf16[4,48,6,6]{3,1,2,0:T(8,128)(2,1)S(1)} %get-tuple-element.9, bf16[4,48,6,6]{3,1,2,0:T(8,128)(2,1)S(1)} %get-tuple-element.10, f32[4,48,6,6]{3,1,2,0:T(8,128)S(1)} %subtract_convert_fusion, ...), kind=kOutput, calls=%fused_computation.20 | convolution fusion | flops 50429952 | bytes 4046976 | tf_op jit(solution)/shard_map/cplub,cludr->cpdrb/dot_general | solution.py:74
  34.3 0.0 slice-start
  34.3 4.5 %pad_maximum_fusion = bf16[4,48,6,6,192]{4,3,1,2,0:T(8,128)(2,1)} fusion(bf16[4,48,6,6,96]{4,3,1,2,0:T(8,128)(2,1)S(1)} %get-tuple-element.6, bf16[4,48,6,6,96]{4,3,1,2,0:T(8,128)(2,1)S(1)} %get-tuple-element.5), kind=kLoop, calls=%fused_computation | loop fusion | flops 5308416 | bytes 5308416 | tf_op jit(solution)/shard_map/concatenate | solution.py:80
  38.8 0.0 collective-permute-done
  38.8 0.0 slice-done
  38.9 0.1 copy.52
  39.0 9.8 %all_gather.7 = bf16[4,192,576]{2,0,1:T(4,128)(2,1)S(1)} all-gather(bf16[4,48,576]{2,0,1:T(4,128)(2,1)S(1)} %copy.52), channel_id=1, replica_groups=mesh['grp'=2,'col'=4,'blk'=4] {'blk'}, dimensions={1}, use_global_device_ids=true | all-gather | bytes 1105920 | tf_op jit(solution)/shard_map/all_gather | solution.py:89
  48.7 1.3 %copy.53 = bf16[4,192,576]{1,2,0:T(8,128)(2,1)S(1)} copy(bf16[4,192,576]{2,0,1:T(4,128)(2,1)S(1)} %all_gather.7) | data formatting | bytes 1769472 | tf_op jit(solution)/shard_map/all_gather | solution.py:89
  50.0 3.7 %fusion.14 = bf16[4,48,6,96]{3,1,2,0:T(8,128)(2,1)S(1)} fusion(bf16[4,48,6,6,192]{4,3,1,2,0:T(8,128)(2,1)} %pad_maximum_fusion, bf16[4,192,6,96]{1,3,2,0:T(8,128)(2,1)S(1)} %bitcast.62, s32[4,192,6]{1,2,0:T(8,128)S(1)} %get-tuple-element.23, pred[4,192]{1,0:T(4,128)(4,1)S(1)} %get-tuple-element.18), kind=kOutput, calls=%fused_computation.15 | convolution fusion | flops 256241664 | bytes 3779328 | tf_op jit(solution)/shard_map/cpdrb,cbre->cpde/dot_general | solution.py:99
  53.7 0.1 copy.56
  53.8 1.0 %reshape.412 = bf16[4,48,576]{2,1,0:T(8,128)(2,1)} reshape(bf16[4,48,6,96]{3,2,1,0:T(8,128)(2,1)S(1)} %copy.56) | data formatting | bytes 442368 | tf_op jit(solution)/shard_map/reshape | solution.py:102
  (13 shorter events, 0.1 us)
Async XLA Ops:
  0.8 38.0 %collective-permute-start = (bf16[1,48,576]{2,1,0:T(8,128)(2,1)S(1)}, bf16[1,48,576]{2,1,0:T(8,128)(2,1)S(1)}, u32[]{:S(2)}, u32[]{:S(2)}) collective-permute-start(bf16[1,48,576]{2,1,0:T(8,128)(2,1)S(1)} %slice.62), channel_id=1, source_target_pairs={{0,12},{4,0},{8,4},{12,8},{1,13},{5,1},{9,5},{13,9},{2,14},{6,2},{... | collective-permute-start | bytes 165896 | tf_op jit(solution)/shard_map/ppermute | solution.py:13
  12.8 12.3 %copy-start = (bf16[4,6,6,6,6]{4,0,3,2,1:T(4,128)(2,1)S(1)}, bf16[4,6,6,6,6]{4,0,3,2,1:T(4,128)(2,1)}, u32[]{:S(2)}) copy-start(bf16[4,6,6,6,6]{4,0,3,2,1:T(4,128)(2,1)} %param.7) | copy-start | bytes 31108
  34.3 4.5 %slice-start = ((bf16[4,48,576]{2,1,0:T(8,128)(2,1)}), bf16[3,48,576]{2,1,0:T(8,128)(2,1)S(1)}, s32[]{:S(2)}) async-start(bf16[4,48,576]{2,1,0:T(8,128)(2,1)} %param.9), calls=%async_computation | async-start | bytes 368640 | tf_op jit(solution)/shard_map/slice | solution.py:88
where the time goes:
time: 55.2 us; the launch traced here: 54.8 us
  blocking collectives  19.6 us (36%)
  matrix products  11.3 us (20%)
  local copies, waits for them, and re-layouts  9.95 us (18%)
  other arithmetic  8.7 us (16%)
  starting transfers between devices  5.08 us (9%)
    all_gather x1, blocking collectives, per_device(): piece = lax.all_gather(boundary, 'blk', axis=1, tiled=True)  9.8 us
    all_gather x1, blocking collectives, per_device(): piece = lax.all_gather(right_next, 'blk', axis=1, tiled=True)  9.78 us
    dot_general x1, matrix products, per_device(): jnp.einsum('cplub,cludr->cpdrb', absorbed, row_m, preferred_element_type=...  6.63 us
    ppermute x1, starting transfers between devices, passed_along(): lax.ppermute(x, axis, [(i, (i + by) % length) for i in range(length)])  5.08 us
    concatenate x1, other arithmetic, per_device(): jnp.concatenate([mixed * (block_par == 0).astype(jnp.bfloat16)[..., None]...  4.46 us
    dot_general x1, matrix products, per_device(): jnp.einsum('cpdrb,cbre->cpde', mixed_dense, piece_m, preferred_element_ty...  3.67 us
    reshape x1, local copies, waits for them, and re-layouts, per_device(): left_proj.reshape(col_dev, sub_rows, D, BLOCK)  1.31 us
    all_gather x1, local copies, waits for them, and re-layouts, per_device(): piece = lax.all_gather(boundary, 'blk', axis=1, tiled=True)  1.27 us
  transfers between devices with their start and end apart: 1, of which 0 were waited for; matrix products, arithmetic and copies ran while one was open for 42% of the time, Pallas kernels for 0%

commit v1 on v0

--- a/solution.py
+++ b/solution.py
@@ -6,6 +6,16 @@
 CHI = 128
 BLOCK = 96
 D = 6
+
+
+def turned_line(x, mesh_axis, along):
+    size = lax.axis_size(mesh_axis)
+    held, tiles = (x, [x])
+    for _ in range(size - 1):
+        held = lax.ppermute(held, mesh_axis, [(i, (i + 1) % size) for i in range(size)])
+        tiles.insert(0, held)
+    line = jnp.concatenate(tiles, axis=along)
+    return jnp.roll(line, (lax.axis_index(mesh_axis) + 1) * x.shape[along], axis=along)
 
 
 def passed_along(x, axis, by):
@@ -86,7 +96,7 @@
     )
     incoming = passed_along(right_proj[:1], "col", -1)
     right_next = jnp.concatenate([right_proj[1:], incoming], axis=0)
-    piece = lax.all_gather(right_next, "blk", axis=1, tiled=True)
+    piece = turned_line(right_next, "blk", 1)
     count_rows = piece.shape[1]
     row_index = lax.iota(jnp.int32, count_rows)
     row_parity = row_index // BLOCK

time: 55.2 us -> 62.8 us (1.14)
  blocking collectives: 19.6 us -> 9.67 us
  local copies, waits for them, and re-layouts: 9.95 us -> 18.1 us
  waiting for transfers between devices: 0.01 us -> 4.86 us
  other arithmetic: 8.7 us -> 10.3 us
  matrix products: 11.3 us -> 12.8 us
  starting transfers between devices: 5.08 us -> 6.4 us
    all_gather x1 -> x0, blocking collectives: 9.78 us -> none  [per_device(): piece = lax.all_gather(right_next, 'blk', axis=1, tiled=True)]
    concatenate x0 -> x1, local copies, waits for them, and re-layouts: none -> 6.45 us  [turned_line(): jnp.roll(line, (lax.axis_index(mesh_axis) + 1) * x.shape[along], axis=along)]
    ppermute x0 -> x3, waiting for transfers between devices: none -> 4.86 us  [turned_line(): lax.ppermute(held, mesh_axis, [(i, (i + 1) % size) for i in range(size)])]
    dynamic_slice x0 -> x1, local copies, waits for them, and re-layouts: none -> 1.82 us  [turned_line(): jnp.roll(line, (lax.axis_index(mesh_axis) + 1) * x.shape[along], axis=along)]
    concatenate x1, other arithmetic: 4.46 us -> 6.09 us  [per_device(): jnp.concatenate([mixed * (block_par == 0).astype(jnp.bfloat16)[..., None]...]
    dot_general x1, matrix products: 6.63 us -> 8.11 us  [per_device(): jnp.einsum('cplub,cludr->cpdrb', absorbed, row_m, preferred_element_type=...]
    ppermute x0 -> x3, starting transfers between devices: none -> 1.32 us  [turned_line(): lax.ppermute(held, mesh_axis, [(i, (i + 1) % size) for i in range(size)])]
    all_gather x1 -> x0, local copies, waits for them, and re-layouts: 1.27 us -> none  [per_device(): piece = lax.all_gather(right_next, 'blk', axis=1, tiled=True)]
  transfers between devices with their start and end apart: 1 -> 4, of which waited for: 0 -> 1; matrix products, arithmetic and copies ran while one was open for 42% -> 43% of each run, Pallas kernels for 0% -> 0%
where the time goes in v1:
time: 62.8 us; the launch traced here: 62.3 us
  local copies, waits for them, and re-layouts  18.1 us (29%)
  matrix products  12.8 us (20%)
  other arithmetic  10.3 us (16%)
  blocking collectives  9.67 us (15%)
  starting transfers between devices  6.4 us (10%)
  waiting for transfers between devices  4.86 us (8%)
    all_gather x1, blocking collectives, per_device(): piece = lax.all_gather(boundary, 'blk', axis=1, tiled=True)  9.67 us
    dot_general x1, matrix products, per_device(): jnp.einsum('cplub,cludr->cpdrb', absorbed, row_m, preferred_element_type=...  8.11 us
    concatenate x1, local copies, waits for them, and re-layouts, turned_line(): jnp.roll(line, (lax.axis_index(mesh_axis) + 1) * x.shape[along], axis=along)  6.45 us
    concatenate x1, other arithmetic, per_device(): jnp.concatenate([mixed * (block_par == 0).astype(jnp.bfloat16)[..., None]...  6.09 us
    ppermute x1, starting transfers between devices, passed_along(): lax.ppermute(x, axis, [(i, (i + by) % length) for i in range(length)])  5.08 us
    ppermute x3, waiting for transfers between devices, turned_line(): lax.ppermute(held, mesh_axis, [(i, (i + 1) % size) for i in range(size)])  4.86 us
    dot_general x1, matrix products, per_device(): jnp.einsum('cpdrb,cbre->cpde', mixed_dense, piece_m, preferred_element_ty...  3.67 us
    dynamic_slice x1, local copies, waits for them, and re-layouts, turned_line(): jnp.roll(line, (lax.axis_index(mesh_axis) + 1) * x.shape[along], axis=along)  1.82 us
  transfers between devices with their start and end apart: 4, of which 1 were waited for; matrix products, arithmetic and copies ran while one was open for 43% of the time, Pallas kernels for 0%

profile of v1, /device:TPU:0, one launch (start us, length us, event | category | flops | bytes accessed | tf_op | source)
XLA Modules:
  0.0 62.3 jit_solution(6424357752129689720)
XLA Ops:
  0.0 0.8 %slice.62 = bf16[1,48,576]{2,1,0:T(8,128)(2,1)S(1)} slice(bf16[4,48,576]{2,1,0:T(8,128)(2,1)} %param.9), slice={[0:1], [0:48], [0:576]} | slice | bytes 110592 | tf_op jit(solution)/shard_map/slice | solution.py:97
  0.8 5.1 %collective-permute-start = (bf16[1,48,576]{2,1,0:T(8,128)(2,1)S(1)}, bf16[1,48,576]{2,1,0:T(8,128)(2,1)S(1)}, u32[]{:S(2)}, u32[]{:S(2)}) collective-permute-start(bf16[1,48,576]{2,1,0:T(8,128)(2,1)S(1)} %slice.62), channel_id=1, source_target_pairs={{0,12},{4,0},{8,4},{12,8},{1,13},{5,1},{9,5},{13,9},{2,14},{6,2},{... | collective-permute-start | bytes 165896 | tf_op jit(solution)/shard_map/ppermute | solution.py:23
  5.9 0.7 %slice.57 = s32[15,2]{0,1:T(2,128)S(1)} slice(s32[16,2]{0,1:T(2,128)} %param.11), slice={[1:16], [0:2]} | slice | bytes 240 | tf_op jit(solution)/shard_map/jit(_roll_static)/slice | solution.py:35
  6.7 0.8 %pad_add_fusion = s32[16,2]{0,1:T(2,128)S(1)} fusion(s32[1,2]{0,1:T(2,128)} %bitcast.75, s32[15,2]{0,1:T(2,128)S(1)} %slice.57), kind=kLoop, calls=%fused_computation.103 | loop fusion | flops 32 | bytes 256 | tf_op jit(solution)/shard_map/jit(_roll_static)/concatenate | solution.py:35
  7.4 0.8 %constant_dynamic-slice_fusion.3 = (s32[4,2]{0,1:T(2,128)S(1)}, s32[4,2]{0,1:T(2,128)S(1)}) fusion(s32[16,2]{0,1:T(2,128)S(1)} %pad_add_fusion, s32[]{:T(128)S(6)} %select_n.189, s32[16,2]{0,1:T(2,128)} %param.11), kind=kLoop, calls=%fused_computation.94 | loop fusion | bytes 132 | tf_op jit(solution)/shard_map/dynamic_slice | solution.py:35
  8.3 0.8 %slice.51 = s32[15,3,6]{0,2,1:T(8,128)S(1)} slice(s32[16,3,6]{0,2,1:T(8,128)} %param.10), slice={[1:16], [0:3], [0:6]} | slice | bytes 2160 | tf_op jit(solution)/shard_map/jit(_roll_static)/slice | solution.py:37
  9.1 0.8 %constant_dynamic-slice_fusion.1 = (s32[4,1,6]{0,2,1:T(8,128)S(1)}, s32[4,1,6]{0,2,1:T(8,128)S(1)}, s32[4,1,6]{0,2,1:T(8,128)S(1)}, s32[4,1,6]{0,2,1:T(8,128)S(1)}) fusion(s32[16,3,6]{0,2,1:T(8,128)} %param.10, s32[]{:T(128)S(6)} %select_n.189, s32[]{:T(128)S(6)} %add.336, s32[]{:T(128)S(6)} %add.337, s32[1,3,6]{0,2,1:T(8,128)} %bitcast.63, ...), kind=kLoop, calls=%fused_computation.92 | loop fusion | flops 24 | bytes 1836 | tf_op jit(solution)/shard_map/slice | solution.py:42
  9.9 0.1 copy.37
  10.0 0.1 copy.41
  10.1 0.1 copy.38
  10.2 0.1 fusion.45
  10.3 0.0 copy-start
  10.3 1.3 %reshape.409 = bf16[4,48,6,96]{3,2,1,0:T(8,128)(2,1)S(1)} reshape(bf16[4,48,576]{2,1,0:T(8,128)(2,1)} %param.8) | data formatting | bytes 442368 | tf_op jit(solution)/shard_map/reshape | solution.py:55
  11.6 0.1 copy.43
  11.7 0.1 copy.39
  11.8 1.0 %copy.46 = bf16[4,48,576]{2,0,1:T(4,128)(2,1)S(1)} copy(bf16[4,48,576]{2,1,0:T(8,128)(2,1)} %param.6) | data formatting | bytes 442368 | tf_op args[0]
  12.9 9.7 %all_gather.3 = bf16[4,192,576]{2,0,1:T(4,128)(2,1)S(1)} all-gather(bf16[4,48,576]{2,0,1:T(4,128)(2,1)S(1)} %copy.46), channel_id=1, replica_groups=mesh['grp'=2,'col'=4,'blk'=4] {'blk'}, dimensions={1}, use_global_device_ids=true | all-gather | bytes 1105920 | tf_op jit(solution)/shard_map/all_gather | solution.py:63
  22.5 1.3 %copy.47 = bf16[4,192,576]{1,2,0:T(8,128)(2,1)S(1)} copy(bf16[4,192,576]{2,0,1:T(4,128)(2,1)S(1)} %all_gather.3) | data formatting | bytes 1769472 | tf_op jit(solution)/shard_map/all_gather | solution.py:63
  23.8 0.1 copy.44
  23.9 0.1 copy.40
  24.0 0.1 copy.42
  24.1 0.1 broadcast_select_fusion
  24.2 0.1 select_compare_fusion.2
  24.3 0.7 %fusion.36 = bf16[4,6,6,6,6,1]{4,0,3,2,1,5:T(4,128)(2,1)S(1)} fusion(bf16[4,6,6,6,6]{4,0,3,2,1:T(4,128)(2,1)S(1)} %copy-done, s32[4,6,6]{0,2,1:T(8,128)S(1)} %get-tuple-element.15, s32[4,6]{1,0:T(4,128)S(1)} %bitcast.64, s32[4,6,6,6]{0,3,2,1:T(8,128)S(1)} %broadcast_add_fusion), kind=kLoop, calls=%fused_computation.52 | loop fusion | flops 98496 | bytes 24864 | tf_op jit(solution)/shard_map/mul | solution.py:83
  25.0 0.1 fusion.41
  25.1 0.1 select_compare_fusion
  25.1 0.6 %broadcast_multiply_fusion.3 = (bf16[4,48,6,96]{3,1,2,0:T(8,128)(2,1)S(1)}, bf16[4,48,6,96]{3,1,2,0:T(8,128)(2,1)S(1)}) fusion(bf16[4,48,6]{1,2,0:T(8,128)(2,1)S(1)} %get-tuple-element.16, bf16[4,48,6,96]{3,2,1,0:T(8,128)(2,1)S(1)} %reshape.409, s32[4,48,6]{1,2,0:T(8,128)S(1)} %get-tuple-element.31, pred[4,48]{1,0:T(4,128)(4,1)S(1)} %select_compare_fusion.2, ...), kind=kLoop, calls=%fused_computation.54 | loop fusion | flops 1105920 | bytes 672960 | tf_op jit(solution)/shard_map/mul | solution.py:58
  25.8 0.0 slice-start
  25.8 1.0 %convert_bitcast_fusion = bf16[4,48,6,6,96,1]{4,1,3,2,0,5:T(8,128)(2,1)S(1)} fusion(bf16[4,192,6,96]{1,3,2,0:T(8,128)(2,1)S(1)} %bitcast.62, s32[4,192,6]{1,2,0:T(8,128)S(1)} %get-tuple-element.24, pred[4,192]{1,0:T(4,128)(4,1)S(1)} %get-tuple-element.19, bf16[4,48,6,96]{3,1,2,0:T(8,128)(2,1)S(1)} %get-tuple-element.8, ...), kind=kOutput, calls=%fused_computation.13 | convolution fusion | flops 257679360 | bytes 2673408 | tf_op jit(solution)/shard_map/cpla,caub->cplub/dot_general | solution.py:73
  26.8 0.4 subtract_convert_fusion
  27.2 0.0 collective-permute-done
  27.2 0.4 collective-permute-start.1
  27.6 0.4 compare_convert_fusion.1
  28.1 4.9 %collective-permute-done.1 = bf16[4,48,576]{2,1,0:T(8,128)(2,1)S(1)} collective-permute-done((bf16[4,48,576]{2,1,0:T(8,128)(2,1)S(1)}, bf16[4,48,576]{2,1,0:T(8,128)(2,1)S(1)}, u32[]{:S(2)}, u32[]{:S(2)}) %collective-permute-start.1) | collective-permute-done | bytes 221216 | tf_op jit(solution)/shard_map/ppermute | solution.py:15
  32.9 0.0 collective-permute-start.2
  32.9 8.1 %broadcast_multiply_fusion.1 = (bf16[4,48,6,6,96]{4,3,1,2,0:T(8,128)(2,1)S(1)}, bf16[4,48,6,6,96]{4,3,1,2,0:T(8,128)(2,1)}) fusion(bf16[4,48,6,6]{3,1,2,0:T(8,128)(2,1)S(1)} %get-tuple-element.9, bf16[4,48,6,6]{3,1,2,0:T(8,128)(2,1)S(1)} %get-tuple-element.10, f32[4,48,6,6]{3,1,2,0:T(8,128)S(1)} %subtract_convert_fusion, ...), kind=kOutput, calls=%fused_computation.20 | convolution fusion | flops 50429952 | bytes 4046976 | tf_op jit(solution)/shard_map/cplub,cludr->cpdrb/dot_general | solution.py:84
  41.0 0.9 %collective-permute-start.3 = (bf16[4,48,576]{2,1,0:T(8,128)(2,1)S(1)}, bf16[4,48,576]{2,1,0:T(8,128)(2,1)S(1)}, u32[]{:S(2)}, u32[]{:S(2)}) collective-permute-start(bf16[4,48,576]{2,1,0:T(8,128)(2,1)S(1)} %collective-permute-done.2), channel_id=1, source_target_pairs={{0,1},{1,2},{2,3},{3,0},{4,5},{5,6},{6,7},{7,4},{8,9},{9,10},{10,1... | collective-permute-start | bytes 663560 | tf_op jit(solution)/shard_map/ppermute | solution.py:15
  41.9 6.1 %pad_maximum_fusion = bf16[4,48,6,6,192]{4,3,1,2,0:T(8,128)(2,1)} fusion(bf16[4,48,6,6,96]{4,3,1,2,0:T(8,128)(2,1)} %get-tuple-element.6, bf16[4,48,6,6,96]{4,3,1,2,0:T(8,128)(2,1)S(1)} %get-tuple-element.5), kind=kLoop, calls=%fused_computation | loop fusion | flops 5308416 | bytes 5308416 | tf_op jit(solution)/shard_map/concatenate | solution.py:90
  48.0 0.3 copy.54
  48.3 0.3 copy.53
  48.7 0.3 copy.52
  49.0 0.0 collective-permute-done.3
  49.0 0.3 copy.51
  49.3 6.5 %concatenate.28 = bf16[4,384,576]{1,2,0:T(8,128)(2,1)} concatenate(bf16[4,48,576]{1,2,0:T(8,128)(2,1)S(1)} %copy.51, bf16[4,48,576]{1,2,0:T(8,128)(2,1)S(1)} %copy.52, bf16[4,48,576]{1,2,0:T(8,128)(2,1)S(1)} %copy.53, bf16[4,48,576]{1,2,0:T(8,128)(2,1)S(1)} %copy.54, bf16[4,48,576]{1,2,0:T(8,128)(2,1)S(1)} %copy.51, bf16[4,48,576]{1,2,0:T(8,128)(2,1)S(1)} %copy.52, ...), dimensions={1} | concatenate | bytes 3538944 | tf_op jit(solution)/shard_map/jit(_roll_dynamic)/concatenate | solution.py:18
  55.7 1.8 %constant_dynamic-slice_fusion.2 = bf16[4,192,576]{1,2,0:T(8,128)(2,1)S(1)} fusion(bf16[4,384,576]{1,2,0:T(8,128)(2,1)} %concatenate.28, s32[]{:T(128)S(6)} %select_n.207), kind=kLoop, calls=%fused_computation.93 | loop fusion | bytes 1769476 | tf_op jit(solution)/shard_map/jit(_roll_dynamic)/dynamic_slice | solution.py:18
  57.5 3.7 %fusion.14 = bf16[4,48,6,96]{3,1,2,0:T(8,128)(2,1)S(1)} fusion(bf16[4,48,6,6,192]{4,3,1,2,0:T(8,128)(2,1)} %pad_maximum_fusion, bf16[4,192,6,96]{1,3,2,0:T(8,128)(2,1)S(1)} %bitcast.61, s32[4,192,6]{1,2,0:T(8,128)S(1)} %get-tuple-element.23, pred[4,192]{1,0:T(4,128)(4,1)S(1)} %get-tuple-element.18), kind=kOutput, calls=%fused_computation.15 | convolution fusion | flops 256241664 | bytes 3779328 | tf_op jit(solution)/shard_map/cpdrb,cbre->cpde/dot_general | solution.py:109
  61.2 0.1 copy.61
  61.3 1.0 %reshape.412 = bf16[4,48,576]{2,1,0:T(8,128)(2,1)} reshape(bf16[4,48,6,96]{3,2,1,0:T(8,128)(2,1)S(1)} %copy.61) | data formatting | bytes 442368 | tf_op jit(solution)/shard_map/reshape | solution.py:112
  (16 shorter events, 0.1 us)
Async XLA Ops:
  0.8 26.3 %collective-permute-start = (bf16[1,48,576]{2,1,0:T(8,128)(2,1)S(1)}, bf16[1,48,576]{2,1,0:T(8,128)(2,1)S(1)}, u32[]{:S(2)}, u32[]{:S(2)}) collective-permute-start(bf16[1,48,576]{2,1,0:T(8,128)(2,1)S(1)} %slice.62), channel_id=1, source_target_pairs={{0,12},{4,0},{8,4},{12,8},{1,13},{5,1},{9,5},{13,9},{2,14},{6,2},{... | collective-permute-start | bytes 165896 | tf_op jit(solution)/shard_map/ppermute | solution.py:23
  10.3 14.0 %copy-start = (bf16[4,6,6,6,6]{4,0,3,2,1:T(4,128)(2,1)S(1)}, bf16[4,6,6,6,6]{4,0,3,2,1:T(4,128)(2,1)}, u32[]{:S(2)}) copy-start(bf16[4,6,6,6,6]{4,0,3,2,1:T(4,128)(2,1)} %param.7) | copy-start | bytes 31108
  25.8 1.4 %slice-start = ((bf16[4,48,576]{2,1,0:T(8,128)(2,1)}), bf16[3,48,576]{2,1,0:T(8,128)(2,1)S(1)}, s32[]{:S(2)}) async-start(bf16[4,48,576]{2,1,0:T(8,128)(2,1)} %param.9), calls=%async_computation | async-start | bytes 368640 | tf_op jit(solution)/shard_map/slice | solution.py:98
  27.2 5.7 %collective-permute-start.1 = (bf16[4,48,576]{2,1,0:T(8,128)(2,1)S(1)}, bf16[4,48,576]{2,1,0:T(8,128)(2,1)S(1)}, u32[]{:S(2)}, u32[]{:S(2)}) collective-permute-start(bf16[4,48,576]{2,1,0:T(8,128)(2,1)S(1)} %pad_maximum_fusion.1), channel_id=1, source_target_pairs={{0,1},{1,2},{2,3},{3,0},{4,5},{5,6},{6,7},{7,4},{8,9},{9,10},{10,1... | collective-permute-start | bytes 663560 | tf_op jit(solution)/shard_map/ppermute | solution.py:15
  32.9 8.1 %collective-permute-start.2 = (bf16[4,48,576]{2,1,0:T(8,128)(2,1)S(1)}, bf16[4,48,576]{2,1,0:T(8,128)(2,1)S(1)}, u32[]{:S(2)}, u32[]{:S(2)}) collective-permute-start(bf16[4,48,576]{2,1,0:T(8,128)(2,1)S(1)} %collective-permute-done.1), channel_id=1, source_target_pairs={{0,1},{1,2},{2,3},{3,0},{4,5},{5,6},{6,7},{7,4},{8,9},{9,10},{10,1... | collective-permute-start | bytes 663560 | tf_op jit(solution)/shard_map/ppermute | solution.py:15
  41.0 7.9 %collective-permute-start.3 = (bf16[4,48,576]{2,1,0:T(8,128)(2,1)S(1)}, bf16[4,48,576]{2,1,0:T(8,128)(2,1)S(1)}, u32[]{:S(2)}, u32[]{:S(2)}) collective-permute-start(bf16[4,48,576]{2,1,0:T(8,128)(2,1)S(1)} %collective-permute-done.2), channel_id=1, source_target_pairs={{0,1},{1,2},{2,3},{3,0},{4,5},{5,6},{6,7},{7,4},{8,9},{9,10},{10,1... | collective-permute-start | bytes 663560 | tf_op jit(solution)/shard_map/ppermute | solution.py:15
